TPU v7x, 128 devices: a whole 4x4x4 slice. The times are simulated.
128 devices in a mesh: expert: 16 (over y, x), mp: 8 (over z, core).
Axes of the slice: x: 4, y: 4, z: 4, core: 2. Of those that a mesh axis runs over, the one named last changes fastest.
Arguments:
- tokens: bfloat16 [2048, 7168], P('expert', 'mp'), may hold values from -0.625 to 0.625
- cotangent: bfloat16 [2048, 8, 2048], P('expert', None, 'mp'), may hold values from -3 to 3
- weights: bfloat16 [32, 7168, 2048], P('expert', 'mp'), may hold values from -0.0625 to 0.0625
- steps: float32 [32, 2048], P('expert', 'mp'), may hold values from 0.002 to 0.02
- expert_ids: int32 [2048, 8], P('expert'), may hold values from 0 to 31, all different within a row; in each aligned block of 128 rows (0 to 127, 128 to 255, ...) at most 64 rows name the same one
Outputs:
- token_grads: bfloat16 [2048, 7168], P('expert', 'mp')
- weight_grads: bfloat16 [32, 7168, 2048], P('expert', 'mp')
- step_grads: float32 [32, 2048], P('expert', 'mp')
Inputs may be any that keep to these rules, and one draw needn't show every extreme that they name: `expert_ids`: each row names 8 different experts; among the 128 rows of one index of the expert axis, no expert is named by more than 64 rows, a bound that some block reaches of them.
All inputs are finite; a program needn't handle non-finite values.
Results may differ from a plain program's by a relative error of at most 0.0058.
Values may be sent and summed in bfloat16 or wider, within the bound.
A program may use at most 128 MiB of HBM per device.

v0:
```python
import math
import jax
import jax.numpy as jnp
from jax import lax
from jax.sharding import PartitionSpec as P

qmax = 7.0
wiggle = 0.9
two_pi = 6.283185307179586


def quantize(weight_f, step_f):
    scaled = weight_f / step_f
    squash = jnp.tanh(scaled / qmax)
    clipped = qmax * squash
    angles = two_pi * clipped
    stair = clipped - wiggle * jnp.sin(angles) / two_pi
    slopes = (1.0 - wiggle * jnp.cos(angles)) * (1.0 - squash * squash)
    return (step_f * stair, slopes, stair - scaled * slopes)


def slot_table(routes_flat, experts, capacity):
    one_hot = (routes_flat[:, None] == jnp.arange(experts, dtype=jnp.int32)[None, :]).astype(
        jnp.int32
    )
    before = jnp.cumsum(one_hot, axis=0) - one_hot
    position = jnp.sum(before * one_hot, axis=1)
    slot_of = routes_flat * capacity + position
    route_count = routes_flat.shape[0]
    source_of = jnp.full((experts * capacity,), route_count, jnp.int32)
    source_of = source_of.at[slot_of].set(jnp.arange(route_count, dtype=jnp.int32))
    return (slot_of, source_of)


def per_device(tokens, cotangent, weights, steps, expert_ids):
    groups = lax.axis_size("expert")
    local_experts = weights.shape[0]
    experts = groups * local_experts
    tok_rows, top_k = expert_ids.shape
    capacity = tok_rows // 2
    width_part = tokens.shape[1]
    slot_of, source_of = slot_table(expert_ids.reshape(-1), experts, capacity)
    token_of = source_of // top_k
    padded_x = jnp.concatenate([tokens, jnp.zeros((1, width_part), tokens.dtype)], axis=0)
    x_slots = padded_x[token_of].reshape(groups, local_experts, capacity, width_part)
    full_steps = lax.all_gather(steps, "mp", axis=1, tiled=True)
    levels, slopes, step_slopes = quantize(weights.astype(jnp.float32), full_steps[:, None, :])
    quantized = levels.astype(jnp.bfloat16)
    part_width = cotangent.shape[2]
    padded_g = jnp.concatenate(
        [
            cotangent.reshape(tok_rows * top_k, part_width),
            jnp.zeros((1, part_width), cotangent.dtype),
        ],
        axis=0,
    )
    g_slots = padded_g[source_of].reshape(groups, local_experts, capacity, part_width)
    x_recv, g_part = (
        lax.all_to_all(x_slots, "expert", split_axis=0, concat_axis=0, tiled=True),
        lax.all_to_all(g_slots, "expert", split_axis=0, concat_axis=0, tiled=True),
    )
    g_recv = lax.all_gather(g_part, "mp", axis=3, tiled=True)
    raw = jnp.einsum("sjcd,sjcf->jdf", x_recv, g_recv, preferred_element_type=jnp.float32)
    weight_out = (raw * slopes).astype(jnp.bfloat16)
    full_width = width_part * lax.axis_size("mp")
    partial_steps = jnp.sum(raw * step_slopes, axis=1)
    step_out = lax.psum_scatter(partial_steps, "mp", scatter_dimension=1, tiled=True) * (
        1.0 / math.sqrt(full_width * qmax)
    )
    back_slots = jnp.einsum(
        "sjcf,jdf->sjcd", g_recv, quantized, preferred_element_type=jnp.float32
    ).astype(jnp.bfloat16)
    returned = lax.all_to_all(back_slots, "expert", split_axis=0, concat_axis=0, tiled=True)
    per_route = returned.reshape(experts * capacity, width_part)[slot_of]
    token_out = (
        per_route.reshape(tok_rows, top_k, width_part)
        .astype(jnp.float32)
        .sum(axis=1)
        .astype(jnp.bfloat16)
    )
    return (token_out, weight_out, step_out)


def solution(mesh):
    return jax.shard_map(
        per_device,
        mesh=mesh,
        in_specs=(
            P("expert", "mp"),
            P("expert", None, "mp"),
            P("expert", "mp", None),
            P("expert", "mp"),
            P("expert", None),
        ),
        out_specs=(P("expert", "mp"), P("expert", "mp", None), P("expert", "mp")),
        check_vma=False,
    )
```

profile of v0, /device:TPU:0, one launch (start us, length us, event | category | flops | bytes accessed | tf_op | source)
XLA Modules:
  0.0 306.8 jit_solution(9049717152482495890)
XLA Ops:
  7.2 0.8 copy.17
  8.2 0.7 broadcast_multiply_fusion
  8.9 9.0 %reduce-window.6 = s32[32,8,128]{2,1,0:T(8,128)S(1)} reduce-window(s32[32,8,128]{2,1,0:T(8,128)S(1)} %fusion.17, s32[]{:T(128)} %constant.43.clone.1), window={size=1x1x128 pad=0_0x0_0x127_0}, to_apply=%region_0.0 | reduce-window | flops 4161536 | bytes 262148 | tf_op jit(solution)/shard_map/reduce-window
  18.0 0.1 copy.19
  18.6 4.3 %scatter_custom_fusion = s32[2048]{0:T(1024)S(1)} fusion(s32[1024]{0:T(1024)S(1)} %bitcast.58, s32[1024]{0:T(1024)S(1)} %iota.11, s32[]{:T(128)} %constant.41.clone.1), kind=kCustom, calls=%fused_computation.44 | custom fusion | bytes 8196 | tf_op jit(solution)/shard_map/scatter | solution.py:31
  23.0 1.1 concatenate.6
  24.1 7.5 %gather_fusion = bf16[2048,256]{1,0:T(8,128)(2,1)S(1)} fusion(bf16[1025,256]{1,0:T(8,128)(2,1)S(1)} %concatenate.6, s32[2048]{0:T(1024)S(1)} %get-tuple-element.6), kind=kCustom, calls=%fused_computation | custom fusion | bytes 2105344 | tf_op jit(solution)/shard_map/gather | solution.py:57
  31.6 24.1 %all_to_all.15 = bf16[16,2,64,256]{3,2,1,0:T(8,128)(2,1)S(1)} all-to-all(bf16[16,2,64,256]{3,2,1,0:T(8,128)(2,1)S(1)} %bitcast.52), channel_id=1, replica_groups=mesh['expert'=16,'mp'=8] {'expert'}, dimensions={0} | all-to-all | bytes 2097152 | tf_op jit(solution)/shard_map/all_to_all | solution.py:60
  55.7 1.1 copy.21
  56.9 9.5 %gather_fusion.2 = bf16[2048,896]{1,0:T(8,128)(2,1)} fusion(bf16[129,896]{1,0:T(8,128)(2,1)S(1)} %concatenate.7, s32[2048]{0:T(1024)S(1)} %get-tuple-element.5), kind=kCustom, calls=%fused_computation.2 | custom fusion | bytes 7348224 | tf_op jit(solution)/shard_map/gather | solution.py:45
  66.3 4.5 %all-to-all-start.2 = ((bf16[16,2,64,896]{3,2,1,0:T(8,128)(2,1)}), bf16[16,2,64,896]{3,2,1,0:T(8,128)(2,1)}, u32[]{:S(2)}, u32[]{:S(2)}) async-start(bf16[16,2,64,896]{3,2,1,0:T(8,128)(2,1)} %bitcast.50), calls=%async_computation.2 | async-start | bytes 7340032 | tf_op jit(solution)/shard_map/all_to_all | solution.py:59
  70.9 13.1 %all_gather.6 = f32[2,2048]{1,0:T(2,128)S(1)} all-gather(f32[2,256]{1,0:T(2,128)S(1)} %copy-done.1), channel_id=1, replica_groups=mesh['expert'=16,'mp'=8] {'mp'}, dimensions={1}, use_global_device_ids=true | all-gather | bytes 18432 | tf_op jit(solution)/shard_map/all_gather | solution.py:46
  84.0 25.2 %all-gather.2.cloned.1.call-done = bf16[16,2,64,2048]{3,2,0,1:T(8,128)(2,1)} async-done(((bf16[16,2,64,256]{3,2,0,1:T(8,128)(2,1)}), bf16[16,2,64,2048]{3,2,0,1:T(8,128)(2,1)}) %all-gather.2.cloned.1.call-update) | async-done | bytes 8388624 | tf_op jit(solution)/shard_map/all_gather | solution.py:62
  109.1 64.9 %convert_bitcast_fusion = bf16[16,2,64,896]{3,2,0,1:T(8,128)(2,1)S(1)} fusion(bf16[16,2,64,2048]{3,2,0,1:T(8,128)(2,1)} %all-gather.2.cloned.1.call-done, f32[2,2048]{1,0:T(2,128)S(1)} %all_gather.6, bf16[2,896,2048]{2,1,0:T(8,128)(2,1)} %param.7), kind=kOutput, calls=%fused_computation.22 | convolution fusion | flops 7551057920 | bytes 19415040 | tf_op jit(solution)/shard_map/sjcf,jdf->sjcd/dot_general | solution.py:70
  174.0 2.2 copy.22
  176.3 6.9 %all-to-all-start.1 = ((bf16[16,2,64,896]{3,2,1,0:T(8,128)(2,1)}), bf16[16,2,64,896]{3,2,1,0:T(8,128)(2,1)}, u32[]{:S(2)}, u32[]{:S(2)}) async-start(bf16[16,2,64,896]{3,2,1,0:T(8,128)(2,1)} %copy.22), calls=%async_computation.1 | async-start | bytes 7340032 | tf_op jit(solution)/shard_map/all_to_all | solution.py:73
  183.1 0.2 reduce-scatter.4.cloned.1.call-start
  183.4 70.7 %fusion.1 = (f32[2,2048]{1,0:T(2,128)S(1)}, bf16[2,896,2048]{2,1,0:T(8,128)(2,1)}) fusion(f32[2,2048]{1,0:T(2,128)S(1)} %all_gather.6, bf16[2,896,2048]{2,1,0:T(8,128)(2,1)} %param.7, bf16[16,2,64,896]{3,2,1,0:T(8,128)(2,1)} %all-to-all-done.2, bf16[16,2,64,2048]{3,2,0,1:T(8,128)(2,1)} %all-gather.2.cloned.1.call-done), kind=kOutput, calls=%fused_computation.7 | convolution fusion | flops 7582248960 | bytes 26771456 | tf_op jit(solution)/shard_map/sjcd,sjcf->jdf/dot_general | solution.py:63
  254.0 1.4 copy.27
  255.5 33.8 %reduce-scatter.4.cloned.1.call-done = f32[256,2]{1,0:T(8,128)} async-done(((f32[2048,2]{1,0:T(8,128)}), f32[256,2]{1,0:T(8,128)}) %reduce-scatter.4.cloned.1.call-update) | async-done | bytes 2064
  289.3 1.0 copy.28
  290.3 0.6 broadcast_multiply_fusion.1
  290.9 7.2 %gather_fusion.1 = bf16[1024,896]{1,0:T(8,128)(2,1)S(1)} fusion(bf16[2048,896]{1,0:T(8,128)(2,1)} %bitcast.9, s32[1024]{0:T(1024)S(1)} %broadcast_clamp_fusion), kind=kCustom, calls=%fused_computation.1 | custom fusion | bytes 3674112 | tf_op jit(solution)/shard_map/gather | solution.py:74
  298.0 1.9 bitcast_reduce_fusion
  (25 shorter events, 0.9 us)
Async XLA Ops:
  7.2 101.9 %all-gather.2.cloned.1.call-start = ((), (), s32[]{:S(2)}) async-start(), calls=%async_computation.4 | async-start | bytes 9437184 | tf_op jit(solution)/shard_map/all_gather | solution.py:62
  17.9 38.9 %copy-start = (bf16[128,896]{1,0:T(8,128)(2,1)S(1)}, bf16[128,896]{1,0:T(8,128)(2,1)}, u32[]{:S(2)}) copy-start(bf16[128,896]{1,0:T(8,128)(2,1)} %param.5) | copy-start | bytes 688132
  56.9 14.0 %copy-start.1 = (f32[2,256]{1,0:T(2,128)S(1)}, f32[2,256]{1,0:T(2,128)}, u32[]{:S(2)}) copy-start(f32[2,256]{1,0:T(2,128)} %param.8) | copy-start | bytes 6148
  66.3 109.9 %all-to-all-start.2 = ((bf16[16,2,64,896]{3,2,1,0:T(8,128)(2,1)}), bf16[16,2,64,896]{3,2,1,0:T(8,128)(2,1)}, u32[]{:S(2)}, u32[]{:S(2)}) async-start(bf16[16,2,64,896]{3,2,1,0:T(8,128)(2,1)} %bitcast.50), calls=%async_computation.2 | async-start | bytes 7340032 | tf_op jit(solution)/shard_map/all_to_all | solution.py:59
  176.3 114.6 %all-to-all-start.1 = ((bf16[16,2,64,896]{3,2,1,0:T(8,128)(2,1)}), bf16[16,2,64,896]{3,2,1,0:T(8,128)(2,1)}, u32[]{:S(2)}, u32[]{:S(2)}) async-start(bf16[16,2,64,896]{3,2,1,0:T(8,128)(2,1)} %copy.22), calls=%async_computation.1 | async-start | bytes 7340032 | tf_op jit(solution)/shard_map/all_to_all | solution.py:73
  183.1 106.1 %reduce-scatter.4.cloned.1.call-start = ((), (), s32[]{:S(2)}) async-start(), calls=%async_computation.5 | async-start | bytes 1179648
Sparse Core Ops, SparseCore 0:
  57.0 52.1 all-gather.1
  255.6 33.6 reduce-scatter.3
where the time goes:
time: 307 us
  matrix products  136 us (44%)
  waiting for transfers between devices  59 us (19%)
  blocking collectives  37.2 us (12%)
  local copies, waits for them, and re-layouts  36.7 us (12%)
  between operations  14.2 us (5%)
  other arithmetic  12.4 us (4%)
  starting transfers between devices  11.7 us (4%)
    dot_general x1, matrix products, per_device(): jnp.einsum('sjcd,sjcf->jdf', x_recv, g_recv, preferred_element_type=jnp.f...  70.7 us
    dot_general x1, matrix products, per_device(): jnp.einsum('sjcf,jdf->sjcd', g_recv, quantized, preferred_element_type=jn...  64.9 us
    unnamed x3, waiting for transfers between devices  33.9 us
    all_gather x1, waiting for transfers between devices, per_device(): g_recv = lax.all_gather(g_part, 'mp', axis=3, tiled=True)  25.2 us
    all_to_all x1, blocking collectives, per_device(): lax.all_to_all(g_slots, 'expert', split_axis=0, concat_axis=0, tiled=True)  24.1 us
    all_gather x1, blocking collectives, per_device(): full_steps = lax.all_gather(steps, 'mp', axis=1, tiled=True)  13.1 us
    gather x1, local copies, waits for them, and re-layouts, per_device(): padded_x[token_of].reshape(groups, local_experts, capacity, width_part)  9.47 us
    another operation x3, other arithmetic  9.15 us
  transfers between devices with their start and end apart: 4, of which 2 were waited for; matrix products, arithmetic and copies ran while one was open for 49% of the time, Pallas kernels for 0%

commit v1 on v0

--- a/solution.py
+++ b/solution.py
@@ -7,6 +7,12 @@
 qmax = 7.0
 wiggle = 0.9
 two_pi = 6.283185307179586
+
+
+def gather_from_all(x, axis, dim):
+    size = lax.axis_size(axis)
+    repeats = [size if d == dim else 1 for d in range(x.ndim)]
+    return lax.all_to_all(jnp.tile(x, repeats), axis, split_axis=dim, concat_axis=dim, tiled=True)
 
 
 def quantize(weight_f, step_f):
@@ -59,7 +65,7 @@
         lax.all_to_all(x_slots, "expert", split_axis=0, concat_axis=0, tiled=True),
         lax.all_to_all(g_slots, "expert", split_axis=0, concat_axis=0, tiled=True),
     )
-    g_recv = lax.all_gather(g_part, "mp", axis=3, tiled=True)
+    g_recv = gather_from_all(g_part, "mp", 3)
     raw = jnp.einsum("sjcd,sjcf->jdf", x_recv, g_recv, preferred_element_type=jnp.float32)
     weight_out = (raw * slopes).astype(jnp.bfloat16)
     full_width = width_part * lax.axis_size("mp")

time: 307 us -> 444 us (1.45)
  blocking collectives: 37.2 us -> 114 us
  other arithmetic: 12.4 us -> 66.8 us
  local copies, waits for them, and re-layouts: 36.7 us -> 80.1 us
  matrix products: 136 us -> 101 us
  waiting for transfers between devices: 59 us -> 51.7 us
    all_gather x1, blocking collectives: 13.1 us -> 89.7 us  [per_device(): full_steps = lax.all_gather(steps, 'mp', axis=1, tiled=True)]
    dot_general x0 -> x1, other arithmetic: none -> 54.3 us  [per_device(): jnp.einsum('sjcf,jdf->sjcd', g_recv, quantized, preferred_element_type=jn...]
    dot_general x1, matrix products: 64.9 us -> 17.7 us  [per_device(): jnp.einsum('sjcf,jdf->sjcd', g_recv, quantized, preferred_element_type=jn...]
    unnamed x7 -> x9, local copies, waits for them, and re-layouts: 3.14 us -> 36.5 us
    all_gather x1 -> x0, waiting for transfers between devices: 25.2 us -> none  [per_device(): g_recv = lax.all_gather(g_part, 'mp', axis=3, tiled=True)]
    all_to_all x1, waiting for transfers between devices: 0.01 us -> 18.5 us  [per_device(): lax.all_to_all(x_slots, 'expert', split_axis=0, concat_axis=0, tiled=True)]
    dot_general x1, matrix products: 70.7 us -> 83.4 us  [per_device(): jnp.einsum('sjcd,sjcf->jdf', x_recv, g_recv, preferred_element_type=jnp.f...]
    another operation x2 -> x3, local copies, waits for them, and re-layouts: 0.08 us -> 6.18 us  [the longest x1 6.1 us: gather_from_all(): jnp.tile(x, repeats)]
  transfers between devices with their start and end apart: 4 -> 4, of which waited for: 2 -> 2; matrix products, arithmetic and copies ran while one was open for 49% -> 43% of each run, Pallas kernels for 0% -> 0%
where the time goes in v1:
time: 444 us; the launch traced here: 443 us
  blocking collectives  114 us (26%)
  matrix products  101 us (23%)
  local copies, waits for them, and re-layouts  80.1 us (18%)
  other arithmetic  66.8 us (15%)
  waiting for transfers between devices  51.7 us (12%)
  starting transfers between devices  14.9 us (3%)
  between operations  14.2 us (3%)
    all_gather x1, blocking collectives, per_device(): full_steps = lax.all_gather(steps, 'mp', axis=1, tiled=True)  89.7 us
    dot_general x1, matrix products, per_device(): jnp.einsum('sjcd,sjcf->jdf', x_recv, g_recv, preferred_element_type=jnp.f...  83.4 us
    dot_general x1, other arithmetic, per_device(): jnp.einsum('sjcf,jdf->sjcd', g_recv, quantized, preferred_element_type=jn...  54.3 us
    unnamed x9, local copies, waits for them, and re-layouts  36.5 us
    unnamed x2, waiting for transfers between devices  33.2 us
    all_to_all x1, blocking collectives, per_device(): lax.all_to_all(g_slots, 'expert', split_axis=0, concat_axis=0, tiled=True)  24.1 us
    all_to_all x1, waiting for transfers between devices, per_device(): lax.all_to_all(x_slots, 'expert', split_axis=0, concat_axis=0, tiled=True)  18.5 us
    dot_general x1, matrix products, per_device(): jnp.einsum('sjcf,jdf->sjcd', g_recv, quantized, preferred_element_type=jn...  17.7 us
  transfers between devices with their start and end apart: 4, of which 2 were waited for; matrix products, arithmetic and copies ran while one was open for 43% of the time, Pallas kernels for 0%

profile of v1, /device:TPU:0, one launch (start us, length us, event | category | flops | bytes accessed | tf_op | source)
XLA Modules:
  0.0 442.5 jit_solution(7369058231346680314)
XLA Ops:
  9.0 9.0 %reduce-window.6 = s32[32,8,128]{2,1,0:T(8,128)S(1)} reduce-window(s32[32,8,128]{2,1,0:T(8,128)S(1)} %fusion.20, s32[]{:T(128)} %constant.43.clone.1), window={size=1x1x128 pad=0_0x0_0x127_0}, to_apply=%region_0.0 | reduce-window | flops 4161536 | bytes 262148 | tf_op jit(solution)/shard_map/reduce-window
  18.6 4.3 scatter_custom_fusion
  22.9 1.1 concatenate.6
  24.0 7.5 %gather_fusion = bf16[2048,256]{1,0:T(8,128)(2,1)S(1)} fusion(bf16[1025,256]{1,0:T(8,128)(2,1)S(1)} %concatenate.6, s32[2048]{0:T(1024)S(1)} %get-tuple-element.6), kind=kCustom, calls=%fused_computation | custom fusion | bytes 2105344 | tf_op jit(solution)/shard_map/gather | solution.py:63
  31.5 24.1 %all_to_all.20 = bf16[16,2,64,256]{3,2,1,0:T(8,128)(2,1)S(1)} all-to-all(bf16[16,2,64,256]{3,2,1,0:T(8,128)(2,1)S(1)} %bitcast.58), channel_id=1, replica_groups=mesh['expert'=16,'mp'=8] {'expert'}, dimensions={0} | all-to-all | bytes 2097152 | tf_op jit(solution)/shard_map/all_to_all | solution.py:66
  55.6 3.1 copy.22
  58.7 6.1 %tile.4 = bf16[16,2,64,8,256]{2,0,1,4,3:T(8,128)(2,1)} broadcast(bf16[16,2,64,256]{2,0,1,3:T(8,128)(2,1)S(1)} %copy.22), dimensions={0,1,2,4} | broadcast | bytes 9437184 | tf_op jit(solution)/shard_map/tile | solution.py:15
  64.8 16.9 %reshape.118 = bf16[8,2,262144]{2,1,0:T(2,128)(2,1)} reshape(bf16[2048,2,16,64]{3,2,1,0:T(8,128)(2,1)} %bitcast.53) | data formatting | bytes 16777216
  81.7 5.3 %all-to-all-start.1 = ((bf16[8,2,262144]{2,1,0:T(2,128)(2,1)}), bf16[8,2,262144]{2,1,0:T(2,128)(2,1)}, u32[]{:S(2)}, u32[]{:S(2)}) async-start(bf16[8,2,262144]{2,1,0:T(2,128)(2,1)} %reshape.118), calls=%async_computation.1 | async-start | bytes 16777216 | tf_op jit(solution)/shard_map/all_to_all | solution.py:15
  87.0 9.5 %gather_fusion.2 = bf16[2048,896]{1,0:T(8,128)(2,1)} fusion(bf16[129,896]{1,0:T(8,128)(2,1)S(1)} %concatenate.7, s32[2048]{0:T(1024)S(1)} %get-tuple-element.5), kind=kCustom, calls=%fused_computation.2 | custom fusion | bytes 7348224 | tf_op jit(solution)/shard_map/gather | solution.py:51
  96.5 89.7 %all_gather.3 = f32[2,2048]{1,0:T(2,128)S(1)} all-gather(f32[2,256]{1,0:T(2,128)S(1)} %copy-done.1), channel_id=1, replica_groups=mesh['expert'=16,'mp'=8] {'mp'}, dimensions={1}, use_global_device_ids=true | all-gather | bytes 18432 | tf_op jit(solution)/shard_map/all_gather | solution.py:52
  186.2 54.3 %fusion.35 = bf16[2,896,2048,1]{2,1,3,0:T(8,128)(2,1)} fusion(f32[2,2048]{1,0:T(2,128)S(1)} %all_gather.3, bf16[2,896,2048]{2,1,0:T(8,128)(2,1)} %param.7), kind=kLoop, calls=%fused_computation.17.clone.clone.clone.clone.1 | loop fusion | flops 33030144 | bytes 14696448 | tf_op jit(solution)/shard_map/sjcf,jdf->sjcd/dot_general | solution.py:76
  240.6 4.7 %all-to-all-start.3 = ((bf16[16,2,64,896]{3,2,1,0:T(8,128)(2,1)}), bf16[16,2,64,896]{3,2,1,0:T(8,128)(2,1)}, u32[]{:S(2)}, u32[]{:S(2)}) async-start(bf16[16,2,64,896]{3,2,1,0:T(8,128)(2,1)} %bitcast.56), calls=%async_computation.3 | async-start | bytes 7340032 | tf_op jit(solution)/shard_map/all_to_all | solution.py:65
  245.3 16.5 %reshape.119 = bf16[2048,2,16,64]{3,2,1,0:T(8,128)(2,1)} reshape(bf16[8,2,262144]{2,1,0:T(2,128)(2,1)} %all-to-all-done.1) | data formatting | bytes 16777216
  261.8 17.7 %convert_bitcast_fusion = bf16[16,2,64,896]{3,2,0,1:T(8,128)(2,1)} fusion(bf16[16,2,64,2048]{2,0,1,3:T(8,128)(2,1)} %bitcast.54, bf16[2,896,2048,1]{2,1,3,0:T(8,128)(2,1)} %fusion.35), kind=kOutput, calls=%fused_computation.23 | convolution fusion | flops 7518027776 | bytes 19398656 | tf_op jit(solution)/shard_map/sjcf,jdf->sjcd/dot_general | solution.py:76
  279.5 4.2 copy.24
  283.7 18.5 %all-to-all-done.3 = bf16[16,2,64,896]{3,2,1,0:T(8,128)(2,1)} async-done(((bf16[16,2,64,896]{3,2,1,0:T(8,128)(2,1)}), bf16[16,2,64,896]{3,2,1,0:T(8,128)(2,1)}, u32[]{:S(2)}, u32[]{:S(2)}) %all-to-all-start.3) | async-done | bytes 3670048 | tf_op jit(solution)/shard_map/all_to_all | solution.py:65
  302.2 4.6 %all-to-all-start.2 = ((bf16[16,2,64,896]{3,2,1,0:T(8,128)(2,1)}), bf16[16,2,64,896]{3,2,1,0:T(8,128)(2,1)}, u32[]{:S(2)}, u32[]{:S(2)}) async-start(bf16[16,2,64,896]{3,2,1,0:T(8,128)(2,1)} %copy.24), calls=%async_computation.2 | async-start | bytes 7340032 | tf_op jit(solution)/shard_map/all_to_all | solution.py:79
  307.1 83.4 %fusion.5 = (f32[2,2048]{1,0:T(2,128)S(1)}, bf16[2,896,2048]{2,1,0:T(8,128)(2,1)}) fusion(f32[2,2048]{1,0:T(2,128)S(1)} %all_gather.3, bf16[2,896,2048]{2,1,0:T(8,128)(2,1)} %param.7, bf16[16,2,64,896]{3,2,1,0:T(8,128)(2,1)} %all-to-all-done.3, bf16[16,2,64,2048]{2,0,1,3:T(8,128)(2,1)} %bitcast.55), kind=kOutput, calls=%fused_computation.11 | convolution fusion | flops 7582248960 | bytes 26771456 | tf_op jit(solution)/shard_map/sjcd,sjcf->jdf/dot_general | solution.py:69
  390.5 1.3 copy.31
  391.8 33.2 %reduce-scatter.4.cloned.1.call-done = f32[256,2]{1,0:T(8,128)} async-done(((f32[2048,2]{1,0:T(8,128)}), f32[256,2]{1,0:T(8,128)}) %reduce-scatter.4.cloned.1.call-update) | async-done | bytes 2064
  425.0 1.0 copy.32
  426.6 7.2 %gather_fusion.1 = bf16[1024,896]{1,0:T(8,128)(2,1)S(1)} fusion(bf16[2048,896]{1,0:T(8,128)(2,1)} %bitcast.10, s32[1024]{0:T(1024)S(1)} %broadcast_clamp_fusion), kind=kCustom, calls=%fused_computation.1 | custom fusion | bytes 3674112 | tf_op jit(solution)/shard_map/gather | solution.py:80
  433.8 1.9 bitcast_reduce_fusion
  (28 shorter events, 3.3 us)
Async XLA Ops:
  64.8 22.2 %copy-start = (bf16[128,896]{1,0:T(8,128)(2,1)S(1)}, bf16[128,896]{1,0:T(8,128)(2,1)}, u32[]{:S(2)}) copy-start(bf16[128,896]{1,0:T(8,128)(2,1)} %param.5) | copy-start | bytes 688132
  81.7 158.9 %all-to-all-start.1 = ((bf16[8,2,262144]{2,1,0:T(2,128)(2,1)}), bf16[8,2,262144]{2,1,0:T(2,128)(2,1)}, u32[]{:S(2)}, u32[]{:S(2)}) async-start(bf16[8,2,262144]{2,1,0:T(2,128)(2,1)} %reshape.118), calls=%async_computation.1 | async-start | bytes 16777216 | tf_op jit(solution)/shard_map/all_to_all | solution.py:15
  87.0 9.5 %copy-start.1 = (f32[2,256]{1,0:T(2,128)S(1)}, f32[2,256]{1,0:T(2,128)}, u32[]{:S(2)}) copy-start(f32[2,256]{1,0:T(2,128)} %param.8) | copy-start | bytes 6148
  240.6 61.6 %all-to-all-start.3 = ((bf16[16,2,64,896]{3,2,1,0:T(8,128)(2,1)}), bf16[16,2,64,896]{3,2,1,0:T(8,128)(2,1)}, u32[]{:S(2)}, u32[]{:S(2)}) async-start(bf16[16,2,64,896]{3,2,1,0:T(8,128)(2,1)} %bitcast.56), calls=%async_computation.3 | async-start | bytes 7340032 | tf_op jit(solution)/shard_map/all_to_all | solution.py:65
  302.2 124.4 %all-to-all-start.2 = ((bf16[16,2,64,896]{3,2,1,0:T(8,128)(2,1)}), bf16[16,2,64,896]{3,2,1,0:T(8,128)(2,1)}, u32[]{:S(2)}, u32[]{:S(2)}) async-start(bf16[16,2,64,896]{3,2,1,0:T(8,128)(2,1)} %copy.24), calls=%async_computation.2 | async-start | bytes 7340032 | tf_op jit(solution)/shard_map/all_to_all | solution.py:79
  306.8 118.2 %reduce-scatter.4.cloned.1.call-start = ((), (), s32[]{:S(2)}) async-start(), calls=%async_computation.5 | async-start | bytes 1179648
Sparse Core Ops, SparseCore 0:
  391.9 33.0 reduce-scatter.3
